TPU v7x, 16 devices: a 4x2x1 block of a 4x4x8 slice. The times are simulated.
16 devices in a mesh: mol: 2 (over y, z), occ: 8 (over x, core).
Axes of the slice: x: 4, y: 2, z: 1, core: 2. Of those that a mesh axis runs over, the one named last changes fastest.
The devices are a block of a 4x4x8 slice.
Arguments:
- b_ints: bfloat16 [672, 80, 152], P(None, ('mol', 'occ')), parts along dimension 1
- eps_occ: float32 [80], P('mol'), parts along dimension 0
- eps_vir: float32 [304], P('mol'), parts along dimension 0
Outputs:
- output 1: float32 [80], P(('mol', 'occ')), parts along dimension 0
- output 2: float32 [2], P('mol'), parts along dimension 0
- output 3: float32 [304, 152], P('mol'), parts along dimension 0
There are 2 independent parts. A program takes and returns all parts, laid end to end along the dimension named above; each array names one.
All inputs are finite; a program needn't handle non-finite values.
Results may differ from a plain program's by a relative error of at most 0.001.
Values are sent between devices in bfloat16 or wider.
A program may use at most 768 MiB of HBM per device.

v0:
```python
import jax
import jax.numpy as jnp
from jax import lax
from jax.sharding import PartitionSpec as P, NamedSharding


def pair_rows(row_b, row_eps, col_b, col_eps, eps_vir, mirror):
    vir_dim = eps_vir.shape[0]
    vir_sum = eps_vir[:, None] + eps_vir[None, :]
    dens_init = jnp.zeros((vir_dim, vir_dim), jnp.float32)
    col_init = jnp.zeros((col_b.shape[1],), jnp.float32)

    def one_row(carry, row_idx):
        dens_acc, col_acc = carry
        b_row = lax.dynamic_index_in_dim(row_b, row_idx, axis=1, keepdims=False)
        k_pair = jnp.einsum('qa,qjb->jab', b_row, col_b, preferred_element_type=jnp.float32)
        e_row = lax.dynamic_index_in_dim(row_eps, row_idx, keepdims=False)
        pair_den = e_row + col_eps[:, None, None] - vir_sum[None]
        t_amp = k_pair / pair_den
        pair_e = jnp.sum(t_amp * (2.0 * k_pair - jnp.swapaxes(k_pair, 1, 2)), axis=(1, 2))
        amp_b = t_amp.astype(jnp.bfloat16)
        mix_b = (2.0 * t_amp - jnp.swapaxes(t_amp, 1, 2)).astype(jnp.bfloat16)
        dens_acc = dens_acc + jnp.einsum('jac,jbc->ab', amp_b, mix_b, preferred_element_type=jnp.float32)
        if mirror:
            dens_acc = dens_acc + jnp.einsum('jca,jcb->ab', amp_b, mix_b, preferred_element_type=jnp.float32)
            col_acc = col_acc + pair_e
        return (dens_acc, col_acc), jnp.sum(pair_e)

    (dens_acc, col_acc), row_acc = lax.scan(one_row, (dens_init, col_init), jnp.arange(row_b.shape[1]))
    return row_acc, col_acc, dens_acc


def mid_block(own_b, own_eps, vis_b, vis_eps, eps_vir, lower):
    blk_rows = own_b.shape[1]
    half_rows = blk_rows // 2

    def low_branch():
        own_part, vis_part, dens_part = pair_rows(own_b[:, :half_rows], own_eps[:half_rows], vis_b, vis_eps, eps_vir, True)
        own_full = jnp.concatenate([own_part, jnp.zeros((blk_rows - half_rows,), jnp.float32)])
        return own_full, vis_part, dens_part

    def up_branch():
        vis_part, own_part, dens_part = pair_rows(vis_b[:, half_rows:], vis_eps[half_rows:], own_b, own_eps, eps_vir, True)
        vis_full = jnp.concatenate([jnp.zeros((half_rows,), jnp.float32), vis_part])
        return own_part, vis_full, dens_part

    return lax.cond(lower, low_branch, up_branch)


def solution(mesh):
    occ_devs = mesh.shape['occ']
    half_span = occ_devs // 2
    shift_perm = [(sender, (sender - 1) % occ_devs) for sender in range(occ_devs)]

    def per_device(b_blk, eps_occ, eps_vir):
        dev_idx = lax.axis_index('occ')
        blk_rows = b_blk.shape[1]
        own_eps = lax.dynamic_slice_in_dim(eps_occ, dev_idx * blk_rows, blk_rows)
        diag_out = pair_rows(b_blk, own_eps, b_blk, own_eps, eps_vir, False)
        own_cred = diag_out[0]
        dens_acc = diag_out[2]
        sent_cred = []
        visitor = b_blk
        for step in range(1, (occ_devs + 1) // 2):
            visitor = lax.ppermute(visitor, 'occ', shift_perm)
            vis_eps = lax.dynamic_slice_in_dim(eps_occ, ((dev_idx + step) % occ_devs) * blk_rows, blk_rows)
            row_cred, col_cred, dens_step = pair_rows(b_blk, own_eps, visitor, vis_eps, eps_vir, True)
            own_cred = own_cred + row_cred
            dens_acc = dens_acc + dens_step
            sent_cred.append(col_cred)
        if occ_devs % 2 == 0:
            visitor = lax.ppermute(visitor, 'occ', shift_perm)
            vis_eps = lax.dynamic_slice_in_dim(eps_occ, ((dev_idx + half_span) % occ_devs) * blk_rows, blk_rows)
            row_cred, col_cred, dens_step = mid_block(b_blk, own_eps, visitor, vis_eps, eps_vir, dev_idx < half_span)
            own_cred = own_cred + row_cred
            dens_acc = dens_acc + dens_step
            sent_cred.append(col_cred)
        zero_cred = jnp.zeros((blk_rows,), jnp.float32)
        by_offset = jnp.stack([own_cred] + sent_cred + [zero_cred] * (occ_devs - 1 - len(sent_cred)))
        by_dest = jnp.roll(by_offset, dev_idx, axis=0)
        e_pair = lax.psum_scatter(by_dest, 'occ', scatter_dimension=0, tiled=True).reshape((blk_rows,))
        energy = lax.psum(jnp.sum(e_pair), 'occ').reshape((1,))
        vir_dens = lax.psum(dens_acc, 'occ')
        return e_pair, energy, vir_dens

    return jax.shard_map(per_device, mesh=mesh, in_specs=(P(None, ('mol', 'occ'), None), P('mol'), P('mol')), out_specs=(P(('mol', 'occ')), P('mol'), P('mol', None)), check_vma=False)
```

profile of v0, /device:TPU:113, one launch (start us, length us, event | category | flops | bytes accessed | tf_op | source)
XLA Modules:
  0.0 307.0 jit_solution(11712331688261687242)
XLA Ops:
  8.9 46.6 %while.88 = (s32[]{:T(128)}, f32[152,152]{1,0:T(8,128)S(1)}, f32[5]{0:T(128)S(1)}, s32[5]{0:T(128)S(1)}, bf16[672,5,152]{0,2,1:T(8,128)(2,1)}, /*index=5*/f32[5]...) while((s32[]{:T(128)}, f32[152,152]{1,0:T(8,128)S(1)}, f32[5]{0:T(128)S(1)}, ...), condition=%wide.region_2.3_spmd.clone, body=%wide.region_0.2_spmd.clone.sunk | while | flops 192294592 | bytes 5468025 | solution.py:29
  13.7 1.9 fusion.180
  23.0 1.9 fusion.180
  32.3 1.9 fusion.180
  41.7 1.9 fusion.180
  51.0 1.9 fusion.180
  56.3 3.4 %collective-permute-start.1 = (bf16[672,5,152]{0,2,1:T(8,128)(2,1)}, bf16[672,5,152]{0,2,1:T(8,128)(2,1)}, u32[]{:S(2)}, u32[]{:S(2)}) collective-permute-start(bf16[672,5,152]{0,2,1:T(8,128)(2,1)} %collective-permute-done), channel_id=1, source_target_pairs={{0,7},{1,0},{2,1},{3,2},{4,3},{5,4},{6,5},{7,6},{8,15},{9,8},{10,9... | collective-permute-start | bytes 3064328 | tf_op jit(solution)/shard_map/ppermute | solution.py:65
  59.7 50.4 %while.89 = (s32[]{:T(128)}, f32[152,152]{1,0:T(8,128)S(1)}, f32[5]{0:T(128)S(1)}, f32[5]{0:T(128)S(1)}, s32[5]{0:T(128)S(1)}, /*index=5*/bf16[672,5,152]{0,2,1:...) while((s32[]{:T(128)}, f32[152,152]{1,0:T(8,128)S(1)}, ...), condition=%wide.region_6.7_spmd.clone, body=%wide.region_3.6_spmd.clone.sunk | while | flops 228706512 | bytes 6761974 | solution.py:29
  64.4 1.9 fusion.189
  74.5 1.9 fusion.189
  84.6 1.9 fusion.189
  94.7 1.9 fusion.189
  104.7 1.9 fusion.189
  110.8 52.6 %while.90 = (s32[]{:T(128)}, f32[152,152]{1,0:T(8,128)S(1)}, f32[5]{0:T(128)S(1)}, f32[5]{0:T(128)S(1)}, s32[5]{0:T(128)S(1)}, /*index=5*/bf16[672,5,152]{0,2,1:...) while((s32[]{:T(128)}, f32[152,152]{1,0:T(8,128)S(1)}, ...), condition=%wide.region_10.11_spmd.clone, body=%wide.region_7.10_spmd.clone.sunk | while | flops 228706512 | bytes 6761974 | solution.py:29
  115.8 1.9 fusion.199
  118.1 1.2 fusion.201
  126.3 1.9 fusion.199
  128.6 1.2 fusion.201
  136.9 1.9 fusion.199
  139.1 1.2 fusion.201
  147.4 1.9 fusion.199
  149.7 1.2 fusion.201
  157.9 1.9 fusion.199
  160.2 1.2 fusion.201
  164.0 50.3 %while.91 = (s32[]{:T(128)}, f32[152,152]{1,0:T(8,128)S(1)}, f32[5]{0:T(128)S(1)}, f32[5]{0:T(128)S(1)}, s32[5]{0:T(128)S(1)}, /*index=5*/bf16[672,5,152]{0,2,1:...) while((s32[]{:T(128)}, f32[152,152]{1,0:T(8,128)S(1)}, ...), condition=%wide.region_14.15_spmd.clone, body=%wide.region_11.14_spmd.clone.sunk | while | flops 228706512 | bytes 6761974 | solution.py:29
  168.8 1.9 fusion.209
  171.0 1.1 fusion.211
  178.8 1.9 fusion.209
  181.1 1.1 fusion.211
  188.9 1.9 fusion.209
  199.0 1.9 fusion.209
  201.3 1.1 fusion.211
  209.1 1.9 fusion.209
  211.3 1.1 fusion.211
  215.0 23.2 %conditional.1 = (f32[5]{0:T(128)S(1)}, f32[152,152]{1,0:T(8,128)}, f32[1,5]{1,0:T(1,128)}) conditional(s32[]{:T(128)} %convert_element_type.39, (bf16[672,5,152]{0,2,1:T(8,128)(2,1)S(1)}, f32[5]{0:T(128)S(1)}, f32[152]{0:T(256)}, bf16[672,5,152]{0,2,1:T(8,128)(2,1)}, f32[5]{0:T(128)S(1)}) %tuple.197, (bf16[672,5,152]{0,2,1:T(8,128)(2,1)}, ...), branch_computations={%region_15.20_spmd, %region_20.25_spmd} | conditional | flops 228706512 | bytes 11930234 | solution.py:47
  216.1 22.1 %while.87 = (s32[]{:T(128)}, f32[152,152]{1,0:T(8,128)}, f32[5]{0:T(128)}, f32[2]{0:T(128)S(1)}, s32[2]{0:T(128)S(1)}, /*index=5*/bf16[672,2,152]{0,2,1:T(8,128)...) while((s32[]{:T(128)}, f32[152,152]{1,0:T(8,128)}, ...), condition=%wide.region_24.24_spmd.clone, body=%wide.region_21.23_spmd.clone.sunk | while | flops 228706512 | bytes 6761974 | solution.py:29
  222.1 1.2 fusion.221
  225.1 1.3 fusion.220
  232.3 1.2 fusion.221
  233.5 1.2 fusion.222
  236.1 2.2 fusion.220
  238.2 1.9 add_add_fusion
  240.3 1.4 concatenate.11
  241.7 19.6 %all-reduce.2 = f32[8,5]{1,0:T(8,128)S(1)} all-reduce(f32[8,5]{1,0:T(8,128)S(1)} %constant_dynamic-slice_fusion.1), channel_id=2, replica_groups=mesh['mol'=2,'occ'=8] {'occ'}, use_global_device_ids=true, to_apply=%region_25.26.clone | all-reduce | flops 40 | bytes 320
  261.2 1.7 fusion.110
  263.0 15.5 %psum.14 = f32[1]{0:T(128)} all-reduce(f32[1]{0:T(128)} %bitcast.7), channel_id=1, replica_groups=mesh['mol'=2,'occ'=8] {'occ'}, use_global_device_ids=true, to_apply=%region_27.28 | all-reduce | flops 1 | bytes 8 | tf_op jit(solution)/shard_map/psum | solution.py:82
  278.4 20.2 %all-reduce.5.cloned.1.call-done = f32[152,152]{1,0:T(8,128)} async-done(((f32[152,152]{1,0:T(8,128)}), f32[152,152]{1,0:T(8,128)}) %all-reduce.5.cloned.1.call-update) | async-done | bytes 92432 | tf_op jit(solution)/shard_map/psum | solution.py:83
  298.6 1.6 copy.187
  (270 shorter events, 127.6 us)
Async XLA Ops:
  7.2 291.4 %all-reduce.5.cloned.1.call-start = ((), (), s32[]{:S(2)}) async-start(), calls=%async_computation | async-start | bytes 311296 | tf_op jit(solution)/shard_map/psum | solution.py:83
  7.2 49.0 %collective-permute-start = (bf16[672,5,152]{0,2,1:T(8,128)(2,1)}, bf16[672,5,152]{0,2,1:T(8,128)(2,1)}, u32[]{:S(2)}, u32[]{:S(2)}) collective-permute-start(bf16[672,5,152]{0,2,1:T(8,128)(2,1)} %param.17), channel_id=1, source_target_pairs={{0,7},{1,0},{2,1},{3,2},{4,3},{5,4},{6,5},{7,6},{8,15},{9,8},{10,9... | collective-permute-start | bytes 3064328 | tf_op jit(solution)/shard_map/ppermute | solution.py:65
  8.9 46.7 %copy-start.8 = (u32[16]{0:T(128)S(1)}, u32[16]{0:T(128)}, u32[]{:S(2)}) copy-start(u32[16]{0:T(128)} %constant.181) | copy-start | bytes 196
  55.6 4.1 %copy-start.5 = (f32[152,152]{1,0:T(8,128)}, f32[152,152]{1,0:T(8,128)S(1)}, u32[]{:S(2)}) copy-start(f32[152,152]{1,0:T(8,128)S(1)} %get-tuple-element.354) | copy-start | bytes 277252
  55.6 4.1 %copy-start.6 = (f32[5]{0:T(128)}, f32[5]{0:T(128)S(1)}, u32[]{:S(2)}) copy-start(f32[5]{0:T(128)S(1)} %get-tuple-element.345) | copy-start | bytes 64
  56.3 53.8 %collective-permute-start.1 = (bf16[672,5,152]{0,2,1:T(8,128)(2,1)}, bf16[672,5,152]{0,2,1:T(8,128)(2,1)}, u32[]{:S(2)}, u32[]{:S(2)}) collective-permute-start(bf16[672,5,152]{0,2,1:T(8,128)(2,1)} %collective-permute-done), channel_id=1, source_target_pairs={{0,7},{1,0},{2,1},{3,2},{4,3},{5,4},{6,5},{7,6},{8,15},{9,8},{10,9... | collective-permute-start | bytes 3064328 | tf_op jit(solution)/shard_map/ppermute | solution.py:65
  110.1 0.7 copy-start.4
  110.1 53.3 %collective-permute-start.2 = (bf16[672,5,152]{0,2,1:T(8,128)(2,1)}, bf16[672,5,152]{0,2,1:T(8,128)(2,1)}, u32[]{:S(2)}, u32[]{:S(2)}) collective-permute-start(bf16[672,5,152]{0,2,1:T(8,128)(2,1)} %collective-permute-done.1), channel_id=1, source_target_pairs={{0,7},{1,0},{2,1},{3,2},{4,3},{5,4},{6,5},{7,6},{8,15},{9,8},{10,9... | collective-permute-start | bytes 3064328 | tf_op jit(solution)/shard_map/ppermute | solution.py:65
  163.3 0.7 copy-start.3
  163.4 51.0 %collective-permute-start.3 = (bf16[672,5,152]{0,2,1:T(8,128)(2,1)}, bf16[672,5,152]{0,2,1:T(8,128)(2,1)S(1)}, u32[]{:S(2)}, u32[]{:S(2)}) collective-permute-start(bf16[672,5,152]{0,2,1:T(8,128)(2,1)} %collective-permute-done.2), channel_id=1, source_target_pairs={{0,7},{1,0},{2,1},{3,2},{4,3},{5,4},{6,5},{7,6},{8,15},{9,8},{10,9... | collective-permute-start | bytes 3064328 | tf_op jit(solution)/shard_map/ppermute | solution.py:72
  214.4 0.7 copy-start.2
  214.4 25.8 %copy-start.7 = (f32[5]{0:T(128)S(1)}, f32[5]{0:T(128)}, u32[]{:S(2)}) copy-start(f32[5]{0:T(128)} %copy-done.6) | copy-start | bytes 64
Sparse Core Ops, SparseCore 0:
  240.4 58.1 all-reduce.4
where the time goes:
time: 311 us; the launch traced here: 307 us
  matrix products  63.8 us (21%)
  other arithmetic  62.6 us (20%)
  local copies, waits for them, and re-layouts  60.6 us (19%)
  loops' own time  45 us (14%)
  blocking collectives  35 us (11%)
  waiting for transfers between devices  20.2 us (6%)
  between operations  14.3 us (5%)
  starting transfers between devices  5.54 us (2%)
    another operation x5, loops' own time, pair_rows(): lax.scan(one_row, (dens_init, col_init), jnp.arange(row_b.shape[1]))  45 us
    dot_general x22, matrix products, one_row(): jnp.einsum('qa,qjb->jab', b_row, col_b, preferred_element_type=jnp.float32)  38.7 us
    reduce_sum x22, other arithmetic, one_row(): return ((dens_acc, col_acc), jnp.sum(pair_e))  24.1 us
    psum x1, waiting for transfers between devices, per_device(): vir_dens = lax.psum(dens_acc, 'occ')  20.2 us
    unnamed x1, blocking collectives  19.6 us
    add x22, other arithmetic, pair_rows(): vir_sum = eps_vir[:, None] + eps_vir[None, :]  18.5 us
    dynamic_update_slice x22, local copies, waits for them, and re-layouts, pair_rows(): lax.scan(one_row, (dens_init, col_init), jnp.arange(row_b.shape[1]))  16.9 us
    dot_general x22, matrix products, one_row(): jnp.einsum('jac,jbc->ab', amp_b, mix_b, preferred_element_type=jnp.float32)  15.8 us
  transfers between devices with their start and end apart: 5, of which 1 were waited for; matrix products, arithmetic and copies ran while one was open for 53% of the time, Pallas kernels for 0%

commit v1 on v0

v1 whole, which is shorter than its diff:
```python
import functools

import jax
import jax.numpy as jnp
from jax import lax
from jax.experimental import pallas as pl
from jax.experimental.pallas import tpu as pltpu
from jax.sharding import PartitionSpec as P

MESH_ID = pl.DeviceIdType.MESH
GROUP = 5
CORES = 2
LANES = 256


def flip(bit, by):
    return lax.rem(bit + by, CORES)


def kernel(n_dev, nb, nv, b_ref, eo_ref, ev_ref, dens_ref, epair_ref, energy_ref,
           blk, kbuf, ktbuf, ucat, wcat, vmat, eacc, dacc, rbuf, gbuf,
           load_sem, sib_sem, nbr_send, n_sem, p_sem, red_send, red_recv, gat_send, gat_recv):
    rows = vmat.shape[0]
    n_chip = n_dev // CORES
    me = lax.axis_index('occ')
    chip, core = me // CORES, lax.rem(me, CORES)
    nxt, prv = lax.rem(chip + 1, n_chip), lax.rem(chip + n_chip - 1, n_chip)
    first = lambda c: jnp.where(c == 0, 1, 0)
    n_src = nxt * CORES + flip(core, first(chip))
    p_src = prv * CORES + flip(core, 1 + first(prv))
    n_dst = prv * CORES + flip(core, first(prv))
    p_dst = nxt * CORES + flip(core, 1 + first(chip))
    sib = chip * CORES + flip(core, 1)
    own0, sib0, n0, p0 = 0, nb, 2 * nb, 3 * nb

    load = pltpu.make_async_copy(b_ref, blk.at[pl.ds(own0, nb)], load_sem)
    load.start()
    barrier = pltpu.get_barrier_semaphore()
    for r in range(1, n_dev):
        pl.semaphore_signal(barrier, inc=1, device_id={'occ': lax.rem(me + r, n_dev)}, device_id_type=MESH_ID)

    kbuf[...] = jnp.zeros_like(kbuf)
    ktbuf[...] = jnp.zeros_like(ktbuf)
    wcat[...] = jnp.zeros_like(wcat)
    eacc[...] = jnp.zeros_like(eacc)
    dacc[...] = jnp.zeros_like(dacc)
    vrow = jnp.broadcast_to(ev_ref[...], (nv, nv))
    vmat[...] = jnp.ones_like(vmat)
    vmat[0:nv, 0:nv] = vrow + vrow.T

    load.wait()
    pl.semaphore_wait(barrier, n_dev - 1)

    def remote(src, dst, send, recv, dev):
        return pltpu.make_async_remote_copy(src_ref=src, dst_ref=dst, send_sem=send, recv_sem=recv,
                                            device_id={'occ': dev}, device_id_type=MESH_ID)

    to_n = [remote(blk.at[own0 + s], blk.at[n0 + s], nbr_send.at[0, s], n_sem.at[s], n_dst) for s in range(nb)]
    to_p = [remote(blk.at[own0 + s], blk.at[p0 + s], nbr_send.at[1, s], p_sem.at[s], p_dst) for s in range(nb)]
    to_s = remote(blk.at[pl.ds(own0, nb)], blk.at[pl.ds(sib0, nb)], sib_sem.at[0], sib_sem.at[1], sib)
    for s in range(nb):
        to_n[s].start()
        to_p[s].start()
        if s == 0:
            to_s.start()

    def orb_energy(slot):
        part, off = slot // nb, lax.rem(slot, nb)
        dev = jnp.where(part == 0, me, jnp.where(part == 1, sib, jnp.where(part == 2, n_src, p_src)))
        return eo_ref[dev * nb + off]

    def work(pairs, diag=False):
        for g, (x, y) in enumerate(pairs):
            k_pair = lax.dot_general(blk[x], blk[y], (((1,), (1,)), ((), ())), preferred_element_type=jnp.float32)
            kbuf[g, 0:nv, 0:nv] = k_pair
            ktbuf[g, 0:nv, 0:nv] = k_pair.T
        for g, (x, y) in enumerate(pairs):
            e_sum = orb_energy(x) + orb_energy(y)
            tot = jnp.zeros((16, LANES), jnp.float32)
            for r0 in range(0, rows, 16):
                rs = pl.ds(r0, 16)
                k, kt = kbuf[g, rs, :], ktbuf[g, rs, :]
                rec = 1.0 / (e_sum - vmat[rs, :])
                t, tt = k * rec, kt * rec
                w, wt = (t + t) - tt, (tt + tt) - t
                tot = tot + k * w
                c0 = 2 * g * LANES
                ucat[rs, c0:c0 + LANES] = t.astype(jnp.bfloat16)
                wcat[pl.ds(c0 + r0, 16), :] = wt.astype(jnp.bfloat16)
                if not diag:
                    c1 = c0 + LANES
                    ucat[rs, c1:c1 + LANES] = tt.astype(jnp.bfloat16)
                    wcat[pl.ds(c1 + r0, 16), :] = w.astype(jnp.bfloat16)
            part = tot[0:8, 0:128] + tot[8:16, 0:128] + tot[0:8, 128:256] + tot[8:16, 128:256]
            eacc[x] = eacc[x] + part
            if not diag:
                eacc[y] = eacc[y] + part
        if diag:
            term = sum(jnp.dot(ucat[:, 2 * g * LANES:(2 * g + 1) * LANES], wcat[2 * g * LANES:(2 * g + 1) * LANES, :],
                               preferred_element_type=jnp.float32) for g in range(len(pairs)))
        else:
            depth = 2 * LANES * len(pairs)
            term = jnp.dot(ucat[:, 0:depth], wcat[0:depth, :], preferred_element_type=jnp.float32)
        dacc[0:rows, :] = dacc[0:rows, :] + term

    work([(own0 + i, own0 + i) for i in range(nb)], diag=True)

    def own_step(i, _):
        work([(own0 + i, own0 + lax.rem(i + d, nb)) for d in range(1, nb // 2 + 1)])
        return 0

    lax.fori_loop(0, nb, own_step, 0)

    to_s.wait_recv()

    def sib_pair(i, d):
        j = lax.rem(i + d, nb)
        return own0 + jnp.where(core == 0, i, j), sib0 + jnp.where(core == 0, j, i)

    half = nb // 2

    def sib_step(i, _):
        work([sib_pair(i, d + jnp.where(core == 0, 0, half + 1)) for d in range(half)])
        return 0

    lax.fori_loop(0, nb, sib_step, 0)

    def sib_rest(i, _):
        work([sib_pair(i, half)])
        return 0

    cut = (nb + 1) // 2
    lax.fori_loop(jnp.where(core == 0, 0, cut), jnp.where(core == 0, cut, nb), sib_rest, 0)

    def step(s, _):
        remote(blk.at[own0], blk.at[n0 + s], nbr_send.at[0, s], n_sem.at[s], n_dst).wait_recv()
        remote(blk.at[own0], blk.at[p0 + s], nbr_send.at[1, s], p_sem.at[s], p_dst).wait_recv()
        work([(own0 + i, n0 + s) for i in range(nb)])
        work([(own0 + i, p0 + s) for i in range(nb)])
        work([(n0 + s, p0 + s)])

        def cross(t, _):
            work([(n0 + s, p0 + t), (n0 + t, p0 + s)])
            return 0

        lax.fori_loop(0, s, cross, 0)
        return 0

    lax.fori_loop(0, nb, step, 0)

    lane = lax.broadcasted_iota(jnp.int32, (8, LANES), 1)
    sub = lax.broadcasted_iota(jnp.int32, (8, LANES), 0)
    erow = jnp.zeros((8, LANES), jnp.float32)
    for part, dev in enumerate((me, sib, n_src, p_src)):
        for s in range(nb):
            e_val = jnp.sum(jnp.sum(eacc[part * nb + s], axis=0, keepdims=True), axis=1, keepdims=True)
            erow = erow + jnp.where((lane == dev * nb + s) & (sub == 0), e_val, 0.0)
    dacc[nv:nv + 8, :] = erow

    cut_rows = gbuf.shape[0] // n_dev
    reds, gats = [], []
    for r in range(1, n_dev):
        dst = lax.rem(me + r, n_dev)
        reds.append(remote(dacc.at[pl.ds(dst * cut_rows, cut_rows)], rbuf.at[r - 1], red_send.at[r - 1], red_recv.at[r - 1], dst))
        reds[-1].start()
    mine = pl.ds(me * cut_rows, cut_rows)
    for c in reds:
        c.wait_recv()
    total = dacc[mine, :]
    for r in range(1, n_dev):
        total = total + rbuf[r - 1]
    gbuf[mine, :] = total
    for r in range(1, n_dev):
        dst = lax.rem(me + r, n_dev)
        gats.append(remote(gbuf.at[mine], gbuf.at[mine], gat_send.at[r - 1], gat_recv.at[r - 1], dst))
        gats[-1].start()
    for r in range(1, n_dev):
        src = lax.rem(me + n_dev - r, n_dev)
        remote(gbuf.at[mine], gbuf.at[pl.ds(src * cut_rows, cut_rows)], gat_send.at[r - 1], gat_recv.at[r - 1], src).wait_recv()
    dens_ref[...] = gbuf[0:nv, 0:nv]
    e_all = gbuf[nv:nv + 8, :]
    energy_ref[...] = jnp.sum(jnp.sum(e_all, axis=0, keepdims=True), axis=1, keepdims=True)
    e_mine = pltpu.roll(e_all, lax.rem(LANES - me * nb, LANES), 1)
    epair_ref[...] = e_mine[0:1, 0:nb]
    for c in to_n + to_p + [to_s] + reds + gats:
        c.wait_send()


def solution(mesh):
    n_dev = mesh.shape['occ']

    def per_device(b_blk, eps_occ, eps_vir):
        nq, nb, nv = b_blk.shape
        rows = (nv + 15) // 16 * 16
        cut_rows = (-(-(nv + 8) // n_dev) + 7) // 8 * 8
        by_orb = jnp.transpose(b_blk, (1, 2, 0))
        vmem = pltpu.VMEM
        dma = pltpu.SemaphoreType.DMA
        dens, e_pair, energy = pl.pallas_call(
            functools.partial(kernel, n_dev, nb, nv),
            out_shape=(jax.ShapeDtypeStruct((nv, nv), jnp.float32), jax.ShapeDtypeStruct((1, nb), jnp.float32),
                       jax.ShapeDtypeStruct((1, 1), jnp.float32)),
            in_specs=[pl.BlockSpec(memory_space=pl.ANY), pl.BlockSpec(memory_space=pltpu.SMEM),
                      pl.BlockSpec(memory_space=vmem)],
            out_specs=(pl.BlockSpec(memory_space=vmem),) * 3,
            scratch_shapes=[
                vmem((4 * nb, nv, nq), jnp.bfloat16),
                vmem((GROUP, rows, LANES), jnp.float32),
                vmem((GROUP, rows, LANES), jnp.float32),
                vmem((rows, 2 * GROUP * LANES), jnp.bfloat16),
                vmem((2 * GROUP * LANES, LANES), jnp.bfloat16),
                vmem((rows, LANES), jnp.float32),
                vmem((4 * nb, 8, 128), jnp.float32),
                vmem((n_dev * cut_rows, LANES), jnp.float32),
                vmem((n_dev - 1, cut_rows, LANES), jnp.float32),
                vmem((n_dev * cut_rows, LANES), jnp.float32),
                dma, dma((2,)), dma((2, nb)), dma((nb,)), dma((nb,)),
                dma((n_dev - 1,)), dma((n_dev - 1,)), dma((n_dev - 1,)), dma((n_dev - 1,)),
            ],
            compiler_params=pltpu.CompilerParams(collective_id=0, has_side_effects=True),
        )(by_orb, eps_occ, eps_vir.reshape(1, nv))
        return e_pair.reshape(nb), energy.reshape(1), dens

    return jax.shard_map(per_device, mesh=mesh, in_specs=(P(None, ('mol', 'occ'), None), P('mol'), P('mol')),
                         out_specs=(P(('mol', 'occ')), P('mol'), P('mol', None)), check_vma=False)
```

time: 311 us -> 53.4 us (0.17); the launches traced: 307 us -> 53.2 us
  matrix products: 63.8 us -> 0 us
  other arithmetic: 62.6 us -> 0 us
  local copies, waits for them, and re-layouts: 60.6 us -> 2.72 us
  Pallas kernels: 0 us -> 48.1 us
  loops' own time: 45 us -> 0 us
  blocking collectives: 35 us -> 0 us
  waiting for transfers between devices: 20.2 us -> 0 us
  between operations: 14.3 us -> 2.39 us
  starting transfers between devices: 5.54 us -> 0 us
    dot_general x61 -> x0, matrix products: 63.8 us -> none  [the longest x22 38.7 us: one_row(): jnp.einsum('qa,qjb->jab', b_row, col_b, preferred_element_type=jnp.float32)]
    pallas_call x0 -> x1, Pallas kernels: none -> 48.1 us  [per_device(): pl.pallas_call(functools.partial(kernel, n_dev, nb, nv), out_shape=(jax.S...]
    another operation x6 -> x0, loops' own time: 45 us -> none  [the longest x5 45 us: pair_rows(): lax.scan(one_row, (dens_init, col_init), jnp.arange(row_b.shape[1]))]
    add x62 -> x0, other arithmetic: 36.8 us -> none  [the longest x22 18.5 us: pair_rows(): vir_sum = eps_vir[:, None] + eps_vir[None, :]]
    dynamic_slice x46 -> x0, local copies, waits for them, and re-layouts: 28 us -> none  [the longest x22 13.6 us: one_row(): e_row = lax.dynamic_index_in_dim(row_eps, row_idx, keepdims=False)]
    reduce_sum x23 -> x0, other arithmetic: 25.8 us -> none  [the longest x22 24.1 us: one_row(): return ((dens_acc, col_acc), jnp.sum(pair_e))]
    psum x1 -> x0, waiting for transfers between devices: 20.2 us -> none  [per_device(): vir_dens = lax.psum(dens_acc, 'occ')]
    unnamed x1 -> x0, blocking collectives: 19.6 us -> none
  transfers between devices with their start and end apart: 5 -> 0, of which waited for: 1 -> 0; matrix products, arithmetic and copies ran while one was open for 53% -> 0% of each run, Pallas kernels for 0% -> 0%
where the time goes in v1:
time: 53.4 us; the launch traced here: 53.2 us
  Pallas kernels  48.1 us (90%)
  local copies, waits for them, and re-layouts  2.72 us (5%)
  between operations  2.39 us (4%)
    pallas_call x1, Pallas kernels, per_device(): pl.pallas_call(functools.partial(kernel, n_dev, nb, nv), out_shape=(jax.S...  48.1 us
    unnamed x2, local copies, waits for them, and re-layouts  2.72 us

profile of v1, /device:TPU:113, one launch (start us, length us, event | category | flops | bytes accessed | tf_op | source)
XLA Modules:
  0.0 53.2 jit_solution(658364171697471865)
XLA Ops:
  0.6 48.1 %shard_map.58 = (f32[152,152]{1,0:T(8,128)}, f32[1,5]{1,0:T(1,128)}, f32[1,1]{1,0:T(1,128)}) custom-call(bf16[5,152,672]{2,1,0:T(8,128)(2,1)} %bitcast.4, f32[40]{0:T(128)} %eo_ref.1, f32[1,152]{1,0:T(1,128)} %bitcast.5), custom_call_target="tpu_custom_call" | custom-call | tf_op jit(solution)/shard_map/pallas_call | solution.py:199
  48.7 1.1 %copy.9 = f32[5]{0:T(128)} copy(f32[5]{0:T(128)} %bitcast.6) | data formatting | bytes 40
  50.5 1.6 %copy.11 = f32[152,152]{1,0:T(8,128)} copy(f32[152,152]{1,0:T(8,128)} %get-tuple-element.14) | data formatting | bytes 184832

commit v2 on v1

v2 whole, which is shorter than its diff:
```python
import functools

import jax
import jax.numpy as jnp
from jax import lax
from jax.experimental import pallas as pl
from jax.experimental.pallas import tpu as pltpu
from jax.sharding import PartitionSpec as P

MESH_ID = pl.DeviceIdType.MESH
CORES = 2
LANES = 128
WIDE = 2 * LANES


def flip(bit, by):
    return lax.rem(bit + by, CORES)


def remote(src, dst, send, recv, dev):
    return pltpu.make_async_remote_copy(src_ref=src, dst_ref=dst, send_sem=send, recv_sem=recv,
                                        device_id={'occ': dev}, device_id_type=MESH_ID)


def kernel(n_dev, nb, nv, nq, b_ref, eo_ref, ev_ref, red_ref, e_ref,
           blk, rem, pack, eo, ev, kbuf, ktbuf, ucat, wcat, vmat, eacc, dacc, part, rbuf, ebuf, elocal,
           load_sem, sib_sem, nbr_send, n_sem, p_sem, red_send, red_recv, gat_send, gat_recv, e_send, e_recv):
    rows = vmat.shape[0]
    main = nq // LANES * LANES
    tail = nq - main
    packed = pack.shape[2]
    n_chip = n_dev // CORES
    me = lax.axis_index('occ')
    chip, core = me // CORES, lax.rem(me, CORES)
    nxt, prv = lax.rem(chip + 1, n_chip), lax.rem(chip + n_chip - 1, n_chip)
    first = lambda c: jnp.where(c == 0, 1, 0)
    n_src = nxt * CORES + flip(core, first(chip))
    p_src = prv * CORES + flip(core, 1 + first(prv))
    n_dst = prv * CORES + flip(core, first(prv))
    p_dst = nxt * CORES + flip(core, 1 + first(chip))
    sib = chip * CORES + flip(core, 1)
    own0, sib0, n0, p0 = 0, nb, 2 * nb, 3 * nb

    barrier = pltpu.get_barrier_semaphore()
    for r in range(1, n_dev):
        pl.semaphore_signal(barrier, inc=1, device_id={'occ': lax.rem(me + r, n_dev)}, device_id_type=MESH_ID)
    loads = [pltpu.make_async_copy(b_ref.at[:, :, main:nq], rem, load_sem.at[0]),
             pltpu.make_async_copy(b_ref.at[:, :, 0:main], blk.at[pl.ds(own0, nb), 0:nv, 0:main], load_sem.at[1]),
             pltpu.make_async_copy(eo_ref, eo, load_sem.at[2]),
             pltpu.make_async_copy(ev_ref, ev, load_sem.at[3])]
    for c in loads:
        c.start()

    for s in range(4 * nb):
        blk[s, nv:rows, :] = jnp.zeros((rows - nv, blk.shape[2]), jnp.bfloat16)
    kbuf[...] = jnp.zeros_like(kbuf)
    ktbuf[...] = jnp.zeros_like(ktbuf)
    wcat[...] = jnp.zeros_like(wcat)
    eacc[...] = jnp.zeros_like(eacc)
    dacc[...] = jnp.zeros_like(dacc)
    part[...] = jnp.zeros_like(part)

    lane = lax.broadcasted_iota(jnp.int32, (packed, LANES), 1)
    groups = LANES // tail
    loads[0].wait()
    for s in range(nb):
        own_tail = jnp.concatenate([rem[s].astype(jnp.float32), jnp.zeros((nv, LANES - tail), jnp.float32)], axis=1)
        blk[own0 + s, 0:nv, main:main + LANES] = own_tail.astype(jnp.bfloat16)
        filled = jnp.concatenate([own_tail, jnp.zeros((groups * packed - nv, LANES), jnp.float32)], axis=0)
        mix = filled[0:packed]
        for g in range(1, groups):
            mix = mix + pltpu.roll(filled[g * packed:(g + 1) * packed], g * tail, 1)
        pack[0, s] = mix.astype(jnp.bfloat16)
    loads[2].wait()
    loads[3].wait()
    vrow = jnp.broadcast_to(ev[...], (nv, nv))
    vmat[...] = jnp.ones_like(vmat)
    vmat[0:nv, 0:nv] = vrow + vrow.T
    loads[1].wait()
    pl.semaphore_wait(barrier, n_dev - 1)

    def cols(slot):
        return blk.at[slot, 0:nv, 0:main]

    to_n = [remote(pack.at[0], pack.at[1], nbr_send.at[0, nb], n_sem.at[nb], n_dst)]
    to_p = [remote(pack.at[0], pack.at[2], nbr_send.at[1, nb], p_sem.at[nb], p_dst)]
    to_s = [remote(pack.at[0], pack.at[3], sib_sem.at[0, 0], sib_sem.at[1, 0], sib),
            remote(blk.at[pl.ds(own0, nb), 0:nv, 0:main], blk.at[pl.ds(sib0, nb), 0:nv, 0:main],
                   sib_sem.at[0, 1], sib_sem.at[1, 1], sib)]
    to_n += [remote(cols(own0 + s), cols(n0 + s), nbr_send.at[0, s], n_sem.at[s], n_dst) for s in range(nb)]
    to_p += [remote(cols(own0 + s), cols(p0 + s), nbr_send.at[1, s], p_sem.at[s], p_dst) for s in range(nb)]
    for s in range(nb + 1):
        to_n[s].start()
        to_p[s].start()
        if s == 1:
            to_s[0].start()
            to_s[1].start()

    def unpack(which, slot0):
        for s in range(nb):
            mix = pack[which, s].astype(jnp.float32)
            parts = [mix] + [pltpu.roll(mix, LANES - g * tail, 1) for g in range(1, groups)]
            full = jnp.concatenate([jnp.where(lane < tail, q, 0.0) for q in parts], axis=0)
            blk[slot0 + s, :, main:main + LANES] = full.astype(jnp.bfloat16)

    def orb_energy(slot):
        if isinstance(slot, int):
            dev = (me, sib, n_src, p_src)[slot // nb]
            return eo[dev * nb + slot % nb]
        kind, off = slot // nb, lax.rem(slot, nb)
        dev = jnp.where(kind == 0, me, jnp.where(kind == 1, sib, jnp.where(kind == 2, n_src, p_src)))
        return eo[dev * nb + off]

    def work(pairs, diag=(), weight=None):
        c0 = 0
        for g, (x, y) in enumerate(pairs):
            k_pair = lax.dot_general(blk[x], blk[y], (((1,), (1,)), ((), ())), preferred_element_type=jnp.float32)
            kbuf[g, :, 0:rows] = k_pair
            ktbuf[g, :, 0:rows] = k_pair.T
            e_sum = orb_energy(x) + orb_energy(y)
            tot = jnp.zeros((16, WIDE), jnp.float32)
            for r0 in range(0, rows, 16):
                rs = pl.ds(r0, 16)
                k, kt = kbuf[g, rs, :], ktbuf[g, rs, :]
                rec = 1.0 / (e_sum - vmat[rs, :])
                if weight is not None and g in weight:
                    rec = rec * weight[g]
                t, tt = k * rec, kt * rec
                w, wt = (t + t) - tt, (tt + tt) - t
                tot = tot + k * w
                ucat[rs, c0:c0 + WIDE] = t.astype(jnp.bfloat16)
                wcat[pl.ds(c0 + r0, 16), :] = wt.astype(jnp.bfloat16)
                if g not in diag:
                    c1 = c0 + WIDE
                    ucat[rs, c1:c1 + WIDE] = tt.astype(jnp.bfloat16)
                    wcat[pl.ds(c1 + r0, 16), :] = w.astype(jnp.bfloat16)
            c0 += WIDE if g in diag else 2 * WIDE
            fold = tot[0:8, 0:LANES] + tot[8:16, 0:LANES] + tot[0:8, LANES:WIDE] + tot[8:16, LANES:WIDE]
            eacc[x] = eacc[x] + fold
            if g not in diag:
                eacc[y] = eacc[y] + fold
        dacc[...] = dacc[...] + jnp.dot(ucat[:, 0:c0], wcat[0:c0, :], preferred_element_type=jnp.float32)

    ring = nb // 2
    work([(own0 + i, own0 + i) for i in range(nb)]
         + [(own0 + i, own0 + (i + d) % nb) for d in range(1, ring + 1) for i in range(nb)], diag=range(nb))

    to_s[0].wait_recv()
    unpack(3, sib0)
    to_s[1].wait_recv()

    def sib_pair(i, d):
        j = lax.rem(i + d, nb)
        return own0 + jnp.where(core == 0, i, j), sib0 + jnp.where(core == 0, j, i)

    shift = jnp.where(core == 0, 0, ring + 1)
    cut = (nb + 1) // 2
    rest = [(jnp.where(core == 0, i, jnp.minimum(cut + i, nb - 1)), ring) for i in range(cut)]
    work([sib_pair(i, d + shift) for d in range(ring) for i in range(nb)] + [sib_pair(i, d) for i, d in rest],
         weight={ring * nb + cut - 1: jnp.where(core == 0, 1.0, 0.0)})

    def arrive(s):
        remote(cols(own0), cols(n0 + s), nbr_send.at[0, s], n_sem.at[s], n_dst).wait_recv()
        remote(cols(own0), cols(p0 + s), nbr_send.at[1, s], p_sem.at[s], p_dst).wait_recv()

    def fresh(s):
        return ([(own0 + i, n0 + s) for i in range(nb)] + [(own0 + i, p0 + s) for i in range(nb)] + [(n0 + s, p0 + s)])

    to_n[0].wait_recv()
    unpack(1, n0)
    to_p[0].wait_recv()
    unpack(2, p0)

    def step(s, _):
        arrive(s)
        work(fresh(s))

        def cross(t, _):
            work([(n0 + s, p0 + t), (n0 + t, p0 + s)])
            return 0

        lax.fori_loop(0, s, cross, 0)
        return 0

    lax.fori_loop(0, nb - 1, step, 0)
    last = nb - 1
    arrive(last)
    work(fresh(last) + [q for t in range(last) for q in ((n0 + last, p0 + t), (n0 + t, p0 + last))])

    extra = nv - LANES
    stack = 32
    part[0:nv, :] = dacc[0:nv, 0:LANES]
    lane32 = lax.broadcasted_iota(jnp.int32, (stack, LANES), 1)
    side = dacc[:, LANES:WIDE]
    mix = side[0:stack]
    for g in range(1, rows // stack):
        mix = mix + pltpu.roll(side[g * stack:(g + 1) * stack], g * extra, 1)
    part[nv:nv + stack, :] = mix

    cut_rows = red_ref.shape[0] // n_dev
    reds, gats, es = [], [], []
    for r in range(1, n_dev):
        dst = lax.rem(me + r, n_dev)
        reds.append(remote(part.at[pl.ds(dst * cut_rows, cut_rows)], rbuf.at[r - 1], red_send.at[r - 1], red_recv.at[r - 1], dst))
        reds[-1].start()

    lane1 = lax.broadcasted_iota(jnp.int32, (1, LANES), 1)
    erow = jnp.zeros((1, LANES), jnp.float32)
    for kind, dev in enumerate((me, sib, n_src, p_src)):
        for s in range(nb):
            e_val = jnp.sum(jnp.sum(eacc[kind * nb + s], axis=0, keepdims=True), axis=1, keepdims=True)
            erow = erow + jnp.where(lane1 == dev * nb + s, e_val, 0.0)
    elocal[...] = erow
    for r in range(1, n_dev):
        es.append(remote(elocal, ebuf.at[r - 1], e_send.at[r - 1], e_recv.at[r - 1], lax.rem(me + r, n_dev)))
        es[-1].start()

    mine = pl.ds(me * cut_rows, cut_rows)
    for c in reds:
        c.wait_recv()
    total = part[mine, :]
    for r in range(1, n_dev):
        total = total + rbuf[r - 1]
    red_ref[mine, :] = total
    for r in range(1, n_dev):
        dst = lax.rem(me + r, n_dev)
        gats.append(remote(red_ref.at[mine], red_ref.at[mine], gat_send.at[r - 1], gat_recv.at[r - 1], dst))
        gats[-1].start()
    for c in es:
        c.wait_recv()
    place = lax.rem(me, n_dev)
    e_all = jnp.zeros((1, LANES), jnp.float32)
    for d in range(n_dev):
        took = elocal[...]
        for r in range(1, n_dev):
            took = jnp.where(lax.rem(place + n_dev - r, n_dev) == d, ebuf[r - 1], took)
        e_all = e_all + took
    e_ref[0:1, :] = pltpu.roll(jnp.broadcast_to(e_all, (8, LANES)), lax.rem(LANES - me * nb, LANES), 1)[0:1]
    e_ref[1:2, :] = jnp.broadcast_to(jnp.sum(e_all, axis=1, keepdims=True), (1, LANES))
    for r in range(1, n_dev):
        src = lax.rem(me + n_dev - r, n_dev)
        remote(red_ref.at[mine], red_ref.at[pl.ds(src * cut_rows, cut_rows)], gat_send.at[r - 1], gat_recv.at[r - 1], src).wait_recv()
    for c in to_n + to_p + to_s + reds + gats + es:
        c.wait_send()


def finish(nb, nv, red_ref, e_ref, dens_ref, epair_ref, energy_ref):
    extra, stack = nv - LANES, 32
    dens_ref[:, 0:LANES] = red_ref[0:nv, :]
    mix = red_ref[nv:nv + stack, :]
    for g in range(-(-nv // stack)):
        n = min(stack, nv - g * stack)
        side = mix if g == 0 else pltpu.roll(mix, LANES - g * extra, 1)
        dens_ref[g * stack:g * stack + n, LANES:nv] = side[0:n, 0:extra]
    epair_ref[...] = e_ref[0:1, 0:nb]
    energy_ref[...] = e_ref[1:2, 0:1]


def solution(mesh):
    n_dev = mesh.shape['occ']

    def per_device(b_blk, eps_occ, eps_vir):
        nq, nb, nv = b_blk.shape
        rows = (nv + 15) // 16 * 16
        n_cut = -(-(nv + 32) // n_dev)
        cut_rows = (n_cut + 7) // 8 * 8
        deep = (nq + LANES - 1) // LANES * LANES
        most = max(3 * nb, 4 * nb - 1)
        by_orb = jnp.transpose(b_blk, (1, 2, 0))
        vmem = pltpu.VMEM
        dma = pltpu.SemaphoreType.DMA
        f32, bf16 = jnp.float32, jnp.bfloat16
        anyspace = pl.BlockSpec(memory_space=pl.ANY)
        in_vmem = pl.BlockSpec(memory_space=vmem)
        red, e_rows = pl.pallas_call(
            functools.partial(kernel, n_dev, nb, nv, nq),
            out_shape=(jax.ShapeDtypeStruct((n_dev * cut_rows, LANES), f32), jax.ShapeDtypeStruct((8, LANES), f32)),
            in_specs=[anyspace] * 3,
            out_specs=(in_vmem,) * 2,
            scratch_shapes=[
                vmem((4 * nb, rows, deep), bf16),
                vmem((nb, nv, nq % LANES), bf16),
                vmem((4, nb, rows // (LANES // (nq % LANES)), LANES), bf16),
                pltpu.SMEM((nb * n_dev,), f32),
                vmem((1, nv), f32),
                vmem((most, rows, WIDE), f32),
                vmem((most, rows, WIDE), f32),
                vmem((rows, 2 * most * WIDE), bf16),
                vmem((2 * most * WIDE, WIDE), bf16),
                vmem((rows, WIDE), f32),
                vmem((4 * nb, 8, LANES), f32),
                vmem((rows, WIDE), f32),
                vmem((n_dev * cut_rows, LANES), f32),
                vmem((n_dev - 1, cut_rows, LANES), f32),
                vmem((n_dev - 1, 1, LANES), f32),
                vmem((1, LANES), f32),
                dma((4,)), dma((2, 2)), dma((2, nb + 1)), dma((nb + 1,)), dma((nb + 1,)),
                dma((n_dev - 1,)), dma((n_dev - 1,)), dma((n_dev - 1,)), dma((n_dev - 1,)),
                dma((n_dev - 1,)), dma((n_dev - 1,)),
            ],
            compiler_params=pltpu.CompilerParams(collective_id=0, has_side_effects=True),
        )(by_orb, eps_occ, eps_vir.reshape(1, nv))
        dens, e_pair, energy = pl.pallas_call(
            functools.partial(finish, nb, nv),
            out_shape=(jax.ShapeDtypeStruct((nv, nv), f32), jax.ShapeDtypeStruct((1, nb), f32), jax.ShapeDtypeStruct((1, 1), f32)),
            in_specs=[in_vmem] * 2,
            out_specs=(in_vmem,) * 3,
        )(red, e_rows)
        return e_pair.reshape(nb), energy.reshape(1), dens

    return jax.shard_map(per_device, mesh=mesh, in_specs=(P(None, ('mol', 'occ'), None), P('mol'), P('mol')),
                         out_specs=(P(('mol', 'occ')), P('mol'), P('mol', None)), check_vma=False)
```

time: 53.4 us -> 44.2 us (0.83)
  Pallas kernels: 48.1 us -> 43.4 us
  local copies, waits for them, and re-layouts: 2.72 us -> 0 us
  between operations: 2.39 us -> 0.64 us
    pallas_call x1 -> x2, Pallas kernels: 48.1 us -> 43.4 us  [the longest x1 41.8 us: per_device(): pl.pallas_call(functools.partial(kernel, n_dev, nb, nv, nq), out_shape=(j...]
    unnamed x2 -> x0, local copies, waits for them, and re-layouts: 2.72 us -> none
where the time goes in v2:
time: 44.2 us; the launch traced here: 44.1 us
  Pallas kernels  43.4 us (98%)
  between operations  0.64 us (1%)
    pallas_call x1, Pallas kernels, per_device(): pl.pallas_call(functools.partial(kernel, n_dev, nb, nv, nq), out_shape=(j...  41.8 us
    pallas_call x1, Pallas kernels, per_device(): pl.pallas_call(functools.partial(finish, nb, nv), out_shape=(jax.ShapeDty...  1.65 us

profile of v2, /device:TPU:113, one launch (start us, length us, event | category | flops | bytes accessed | tf_op | source)
XLA Modules:
  0.0 44.1 jit_solution(2468242966650797016)
XLA Ops:
  0.6 41.8 %shard_map.58 = (f32[192,128]{1,0:T(8,128)}, f32[8,128]{1,0:T(8,128)}) custom-call(bf16[5,152,672]{2,1,0:T(8,128)(2,1)} %bitcast.4, f32[40]{0:T(128)} %eo_ref.1, f32[1,152]{1,0:T(1,128)} %bitcast.5), custom_call_target="tpu_custom_call" | custom-call | tf_op jit(solution)/shard_map/pallas_call | solution.py:275
  42.4 1.6 %shard_map.59 = (f32[152,152]{1,0:T(8,128)}, f32[1,5]{1,0:T(1,128)}, f32[1,1]{1,0:T(1,128)}) custom-call(f32[192,128]{1,0:T(8,128)} %get-tuple-element.8.red_ref, f32[8,128]{1,0:T(8,128)} %get-tuple-element.9.e_ref), custom_call_target="tpu_custom_call" | custom-call | tf_op jit(solution)/shard_map/pallas_call | solution.py:303
